TPU v7x, 256 devices: a whole 4x4x8 slice. The times are simulated.
256 devices in a mesh: blk: 128 (over y_hi, x, z, core), grp: 2 (over y_lo).
Axes of the slice: x: 4, y: 4 (y_hi: 2, y_lo: 2; y = y_hi * 2 + y_lo), z: 8, core: 2. Of those that a mesh axis runs over, the one named last changes fastest.
Arguments:
- embeddings: bfloat16 [262144, 1024], P(('blk', 'grp')), may hold values from -6 to 6
Outputs:
- tile_max: float32 [262144, 40], P(('blk', 'grp'))
All inputs are finite; a program needn't handle non-finite values.
Results may differ from a plain program's by a relative error of at most 0.0017.
Values may be sent and summed in bfloat16 or wider, within the bound.
A program may use at most 64 MiB of HBM per device.

v0:
```python
import jax
import jax.numpy as jnp
from jax import lax
from jax.sharding import PartitionSpec as P


def from_behind(block, axis, distance):
    devices = range(lax.axis_size(axis))
    route = [((i - distance) % len(devices), i) for i in devices]
    return lax.ppermute(block, axis, route)


def tile_rows(scores):
    count = scores.shape[0]
    return jnp.max(scores.reshape(count, count // 128, 128), axis=-1)


def tile_columns(scores):
    count = scores.shape[0]
    return jnp.transpose(jnp.max(scores.reshape(count // 128, 128, count), axis=1))


def body(embeddings):
    count, width = embeddings.shape
    values = embeddings.astype(jnp.float32)
    unit = (values * lax.rsqrt(jnp.mean(values * values, axis=-1, keepdims=True) + 1e-06)).astype(
        jnp.bfloat16
    )
    scale = 1.0 / width**0.5

    def score(keys):
        return (
            lax.dot_general(
                unit, keys, (((1,), (1,)), ((), ())), preferred_element_type=jnp.float32
            )
            * scale
        )

    upper_one = from_behind(unit, ("blk", "grp"), -1)
    upper_two = from_behind(unit, ("blk", "grp"), -2)
    same = jnp.arange(count)[:, None] == jnp.arange(count)[None, :]
    own_max = tile_rows(jnp.where(same, -jnp.inf, score(unit)))
    score_one = score(upper_one)
    score_two = score(upper_two)
    lower_one = from_behind(tile_columns(score_one), ("blk", "grp"), 1)
    lower_two = from_behind(tile_columns(score_two), ("blk", "grp"), 2)
    return jnp.concatenate(
        [lower_two, lower_one, own_max, tile_rows(score_one), tile_rows(score_two)], axis=1
    )


def solution(mesh):
    return jax.shard_map(
        body,
        mesh=mesh,
        in_specs=(P(("blk", "grp"), None),),
        out_specs=P(("blk", "grp"), None),
        check_vma=False,
    )
```

profile of v0, /device:TPU:16, one launch (start us, length us, event | category | flops | bytes accessed | tf_op | source)
XLA Modules:
  0.0 103.5 jit_solution(11567310089639399520)
XLA Ops:
  0.0 2.1 %fusion = f32[1024]{0:T(1024)S(1)} fusion(bf16[1024,1024]{1,0:T(8,128)(2,1)} %param.1), kind=kLoop, calls=%fused_computation.2 | loop fusion | flops 3144704 | bytes 2101248 | tf_op jit(solution)/shard_map/reduce_sum | solution.py:26
  2.1 2.0 %fusion.1 = bf16[1024,1024]{1,0:T(8,128)(2,1)S(1)} fusion(bf16[1024,1024]{1,0:T(8,128)(2,1)} %param.1, f32[1024]{0:T(1024)S(1)} %add_rsqrt_fusion), kind=kLoop, calls=%fused_computation.3 | loop fusion | flops 3145728 | bytes 4198400 | tf_op jit(solution)/shard_map/convert_element_type | solution.py:26
  4.1 7.3 %collective-permute-start = (bf16[1024,1024]{1,0:T(8,128)(2,1)S(1)}, bf16[1024,1024]{1,0:T(8,128)(2,1)}, u32[]{:S(2)}, u32[]{:S(2)}) collective-permute-start(bf16[1024,1024]{1,0:T(8,128)(2,1)S(1)} %fusion.1), channel_id=1, source_target_pairs={{2,0},{3,1},{4,2},{5,3},{6,4},{7,5},{8,6},{9,7},{10,8},{11,9},{12,... | collective-permute-start | bytes 6291464 | tf_op jit(solution)/shard_map/ppermute | solution.py:10
  11.4 0.8 collective-permute-start.2
  12.2 2.4 %select_bitcast_fusion = f32[128,8,8,128]{3,1,2,0:T(8,128)S(1)} fusion(bf16[1024,1024]{1,0:T(8,128)(2,1)S(1)} %fusion.1), kind=kOutput, calls=%fused_computation.6 | convolution fusion | flops 2150629376 | bytes 6291456 | tf_op jit(solution)/shard_map/dot_general | solution.py:33
  14.6 3.0 %copy.10 = f32[128,8,8,128]{3,2,1,0:T(8,128)} copy(f32[128,8,8,128]{3,1,2,0:T(8,128)S(1)} %select_bitcast_fusion) | data formatting | bytes 8388608
  17.5 3.4 %reduce_max.47 = f32[1024,8]{1,0:T(8,128)S(1)} reduce(f32[1024,8,128]{2,1,0:T(8,128)} %bitcast.20, f32[]{:T(128)} %constant.10.clone.1), dimensions={2}, to_apply=%region_3.4 | reduce | flops 1040384 | bytes 4227076 | tf_op jit(solution)/shard_map/reduce_max | solution.py:15
  20.9 0.2 copy.6
  21.1 13.9 %collective-permute-done = bf16[1024,1024]{1,0:T(8,128)(2,1)} collective-permute-done((bf16[1024,1024]{1,0:T(8,128)(2,1)S(1)}, bf16[1024,1024]{1,0:T(8,128)(2,1)}, u32[]{:S(2)}, u32[]{:S(2)}) %collective-permute-start) | collective-permute-done | bytes 2097184 | tf_op jit(solution)/shard_map/ppermute | solution.py:10
  35.0 4.0 %bitcast_reduce_fusion.1 = (f32[8,1024]{1,0:T(8,128)S(1)}, f32[1024,1024]{1,0:T(8,128)S(1)}) fusion(bf16[1024,1024]{1,0:T(8,128)(2,1)S(1)} %fusion.1, bf16[1024,1024]{1,0:T(8,128)(2,1)} %collective-permute-done), kind=kOutput, calls=%fused_computation.5 | convolution fusion | flops 2149572608 | bytes 8421376 | tf_op jit(solution)/shard_map/dot_general | solution.py:33
  39.0 0.3 collective-permute-start.1
  39.2 19.8 %collective-permute-done.2 = bf16[1024,1024]{1,0:T(8,128)(2,1)} collective-permute-done((bf16[1024,1024]{1,0:T(8,128)(2,1)S(1)}, bf16[1024,1024]{1,0:T(8,128)(2,1)}, u32[]{:S(2)}, u32[]{:S(2)}) %collective-permute-start.2) | collective-permute-done | bytes 2097184 | tf_op jit(solution)/shard_map/ppermute | solution.py:10
  59.1 5.9 %bitcast_reduce_fusion = (f32[8,1024]{1,0:T(8,128)S(1)}, f32[1024,1024]{1,0:T(8,128)}) fusion(bf16[1024,1024]{1,0:T(8,128)(2,1)S(1)} %fusion.1, bf16[1024,1024]{1,0:T(8,128)(2,1)} %collective-permute-done.2), kind=kOutput, calls=%fused_computation.4 | convolution fusion | flops 2149572608 | bytes 8421376 | tf_op jit(solution)/shard_map/dot_general | solution.py:33
  64.9 3.0 %copy.12 = f32[128,8,8,128]{3,2,1,0:T(8,128)} copy(f32[128,8,8,128]{3,1,2,0:T(8,128)S(1)} %bitcast.22) | data formatting | bytes 8388608
  67.9 3.4 %reduce_max.49 = f32[1024,8]{1,0:T(8,128)S(1)} reduce(f32[1024,8,128]{2,1,0:T(8,128)} %bitcast.21, f32[]{:T(128)} %constant.10.clone.1), dimensions={2}, to_apply=%region_5.6 | reduce | flops 1040384 | bytes 4227076 | tf_op jit(solution)/shard_map/reduce_max | solution.py:15
  71.3 0.2 copy.8
  71.5 5.2 %copy.11 = f32[128,8,8,128]{3,2,1,0:T(8,128)} copy(f32[128,8,8,128]{3,1,2,0:T(8,128)} %bitcast.23) | data formatting | bytes 8388608
  76.6 3.4 %reduce_max.48 = f32[1024,8]{1,0:T(8,128)S(1)} reduce(f32[1024,8,128]{2,1,0:T(8,128)} %bitcast.19, f32[]{:T(128)} %constant.10.clone.1), dimensions={2}, to_apply=%region_4.5 | reduce | flops 1040384 | bytes 4227076 | tf_op jit(solution)/shard_map/reduce_max | solution.py:15
  80.0 0.2 copy.7
  80.2 3.0 %collective-permute-start.3 = (f32[1024,8]{0,1:T(8,128)S(1)}, f32[1024,8]{0,1:T(8,128)S(1)}, u32[]{:S(2)}, u32[]{:S(2)}) collective-permute-start(f32[1024,8]{0,1:T(8,128)S(1)} %bitcast.25), channel_id=1, source_target_pairs={{255,0},{0,1},{1,2},{2,3},{3,4},{4,5},{5,6},{6,7},{7,8},{8,9},{9,1... | collective-permute-start | bytes 98312 | tf_op jit(solution)/shard_map/ppermute | solution.py:10
  83.2 19.0 %collective-permute-done.3 = f32[1024,8]{0,1:T(8,128)S(1)} collective-permute-done((f32[1024,8]{0,1:T(8,128)S(1)}, f32[1024,8]{0,1:T(8,128)S(1)}, u32[]{:S(2)}, u32[]{:S(2)}) %collective-permute-start.3) | collective-permute-done | bytes 32800 | tf_op jit(solution)/shard_map/ppermute | solution.py:10
  102.2 0.0 copy-start
  102.2 0.7 copy-done
  102.9 0.6 constant_dynamic-update-slice_fusion
  (6 shorter events, 0.0 us)
Async XLA Ops:
  4.1 30.9 %collective-permute-start = (bf16[1024,1024]{1,0:T(8,128)(2,1)S(1)}, bf16[1024,1024]{1,0:T(8,128)(2,1)}, u32[]{:S(2)}, u32[]{:S(2)}) collective-permute-start(bf16[1024,1024]{1,0:T(8,128)(2,1)S(1)} %fusion.1), channel_id=1, source_target_pairs={{2,0},{3,1},{4,2},{5,3},{6,4},{7,5},{8,6},{9,7},{10,8},{11,9},{12,... | collective-permute-start | bytes 6291464 | tf_op jit(solution)/shard_map/ppermute | solution.py:10
  11.4 47.6 %collective-permute-start.2 = (bf16[1024,1024]{1,0:T(8,128)(2,1)S(1)}, bf16[1024,1024]{1,0:T(8,128)(2,1)}, u32[]{:S(2)}, u32[]{:S(2)}) collective-permute-start(bf16[1024,1024]{1,0:T(8,128)(2,1)S(1)} %fusion.1), channel_id=1, source_target_pairs={{1,0},{2,1},{3,2},{4,3},{5,4},{6,5},{7,6},{8,7},{9,8},{10,9},{11,1... | collective-permute-start | bytes 6291464 | tf_op jit(solution)/shard_map/ppermute | solution.py:10
  39.0 44.2 %collective-permute-start.1 = (f32[1024,8]{0,1:T(8,128)S(1)}, f32[1024,8]{0,1:T(8,128)S(1)}, u32[]{:S(2)}, u32[]{:S(2)}) collective-permute-start(f32[1024,8]{0,1:T(8,128)S(1)} %bitcast.24), channel_id=1, source_target_pairs={{254,0},{255,1},{0,2},{1,3},{2,4},{3,5},{4,6},{5,7},{6,8},{7,9},{8... | collective-permute-start | bytes 98312 | tf_op jit(solution)/shard_map/ppermute | solution.py:10
  80.2 22.0 %collective-permute-start.3 = (f32[1024,8]{0,1:T(8,128)S(1)}, f32[1024,8]{0,1:T(8,128)S(1)}, u32[]{:S(2)}, u32[]{:S(2)}) collective-permute-start(f32[1024,8]{0,1:T(8,128)S(1)} %bitcast.25), channel_id=1, source_target_pairs={{255,0},{0,1},{1,2},{2,3},{3,4},{4,5},{5,6},{6,7},{7,8},{8,9},{9,1... | collective-permute-start | bytes 98312 | tf_op jit(solution)/shard_map/ppermute | solution.py:10
  102.2 0.7 copy-start
where the time goes:
time: 105 us; the launch traced here: 103 us
  waiting for transfers between devices  52.7 us (50%)
  other arithmetic  14.2 us (14%)
  local copies, waits for them, and re-layouts  12.9 us (12%)
  matrix products  12.2 us (12%)
  starting transfers between devices  11.4 us (11%)
    ppermute x4, waiting for transfers between devices, from_behind(): return lax.ppermute(block, axis, route)  52.7 us
    dot_general x3, matrix products, score(): lax.dot_general(unit, keys, (((1,), (1,)), ((), ())), preferred_element_t...  12.2 us
    unnamed x9, local copies, waits for them, and re-layouts  11.8 us
    ppermute x4, starting transfers between devices, from_behind(): return lax.ppermute(block, axis, route)  11.4 us
    reduce_max x3, other arithmetic, tile_rows(): return jnp.max(scores.reshape(count, count // 128, 128), axis=-1)  10.1 us
  transfers between devices with their start and end apart: 4, of which 3 were waited for; matrix products, arithmetic and copies ran while one was open for 33% of the time, Pallas kernels for 0%

commit v1 on v0

v1 whole, which is shorter than its diff:
```python
import functools

import jax
import jax.numpy as jnp
from jax import lax
from jax.experimental import pallas as pl
from jax.experimental.pallas import tpu as pltpu
from jax.sharding import PartitionSpec as P

MESH = pl.DeviceIdType.MESH
ROWS = 1024
TILE = 128
TILES = ROWS // TILE
GRP = 2
BLOCKS = 256


def where_of(block):
    block = lax.rem(block + BLOCKS, BLOCKS)
    return (lax.div(block, GRP), lax.rem(block, GRP))


def unit_rows(raw):
    values = raw.astype(jnp.float32)
    return (values * lax.rsqrt(jnp.mean(values * values, axis=-1, keepdims=True) + 1e-06)).astype(
        jnp.bfloat16
    )


def kernel(
    x_ref,
    out_ref,
    raw,
    unit,
    near,
    far,
    extra,
    back,
    load_sem,
    send_sem,
    near_sem,
    far_sem,
    extra_sem,
    back_send_sem,
    back_sem,
):
    b = lax.axis_index("blk") * GRP + lax.axis_index("grp")
    m = lax.rem(b, 4)
    z = lax.rem(lax.div(b, 4), 8)
    x = lax.rem(lax.div(b, 32), 4)
    scale = 1.0 / 1024**0.5

    is_e = x >= 2
    s = jnp.where(is_e, -1, 1)
    role = jnp.where(is_e, 3 - m, m)
    even = lax.rem(role, 2) == 0
    odd = jnp.logical_not(even)
    first_o = jnp.logical_and(x == 0, z == 0)
    first_e = jnp.logical_and(x == 2, z == 0)
    last_e = jnp.logical_and(x == 3, z == 7)
    low = m < 2

    mate = b + 1 - 2 * lax.rem(m, 2)
    no_far = jnp.logical_and(first_e, low)
    has_far = jnp.logical_not(no_far)
    no_send = jnp.logical_or(
        jnp.logical_and(first_o, low), jnp.logical_and(last_e, jnp.logical_not(low))
    )
    sends_far = jnp.logical_not(no_send)
    cross_e = jnp.logical_and(last_e, m == 3)
    cross_o = jnp.logical_and(first_o, m == 0)
    cross = jnp.logical_or(cross_e, cross_o)
    over = jnp.where(is_e, b + 1, b - 1)

    load = pltpu.make_async_copy(x_ref, raw, load_sem)
    load.start()

    barrier = pltpu.get_barrier_semaphore()

    def greet(block):
        pl.semaphore_signal(barrier, inc=1, device_id=where_of(block), device_id_type=MESH)

    greet(mate)
    greet(b + 2 * s)

    @pl.when(sends_far)
    def _():
        greet(b - 2 * s)

    @pl.when(cross)
    def _():
        greet(over)

    count = 2 + sends_far.astype(jnp.int32) + cross.astype(jnp.int32)
    pl.semaphore_wait(barrier, count)
    load.wait()

    def block_copy(dst, sems, which, t, block):
        rows = pl.ds(pl.multiple_of(t * TILE, TILE), TILE)
        return pltpu.make_async_remote_copy(
            src_ref=raw.at[rows],
            dst_ref=dst.at[rows],
            send_sem=send_sem.at[which, t],
            recv_sem=sems.at[t],
            device_id=where_of(block),
            device_id_type=MESH,
        )

    def each_tile(body):
        def step(t, carry):
            body(t)
            return carry

        lax.fori_loop(0, TILES, step, 0)

    def send_all(cond, dst, sems, which, block):
        @pl.when(cond)
        def _():
            each_tile(lambda t: block_copy(dst, sems, which, t, block).start())

    def settle(cond, dst, sems, which, block):
        @pl.when(cond)
        def _():
            each_tile(lambda t: block_copy(dst, sems, which, t, block).wait_send())

    sends = [
        (odd, near, near_sem, 0, mate),
        (sends_far, far, far_sem, 1, b - 2 * s),
        (no_far, far, far_sem, 2, b + 2 * s),
        (cross, extra, extra_sem, 3, over),
    ]
    for send in sends:
        send_all(*send)

    def make_unit(t):
        rows = pl.ds(pl.multiple_of(t * TILE, TILE), TILE)
        unit[rows, :] = unit_rows(raw[rows, :])

    each_tile(make_unit)

    def scores(left, right):
        return lax.dot_general(
            left, right, (((1,), (1,)), ((), ())), preferred_element_type=jnp.float32
        )

    def own_tile(t):
        rows = pl.ds(pl.multiple_of(t * TILE, TILE), TILE)
        left = unit[rows, :]
        for n in range(4):
            block = scores(left, unit[n * 256 : n * 256 + 256, :])
            at = lax.broadcasted_iota(jnp.int32, (TILE, 256), 0) + t * TILE
            to = lax.broadcasted_iota(jnp.int32, (TILE, 256), 1) + n * 256
            block = jnp.where(at == to, -jnp.inf, block)
            out_ref[pl.ds(16 + t, 1), n * 256 : n * 256 + 256] = (
                jnp.max(block, axis=0, keepdims=True) * scale
            )

    each_tile(own_tile)

    def pair_tile(left, rows_ref, t, by_row, row_base, by_key, key_base):
        columns = pl.ds(pl.multiple_of(t * TILE, TILE), TILE)
        for n in range(4):
            block = scores(left, rows_ref[n * 256 : n * 256 + 256, :])
            by_row[pl.ds(row_base + t, 1), n * 256 : n * 256 + 256] = (
                jnp.max(block, axis=0, keepdims=True) * scale
            )
            for h in range(2):
                turned = jnp.transpose(block[:, h * 128 : h * 128 + 128])
                by_key[pl.ds(key_base + 2 * n + h, 1), columns] = (
                    jnp.max(turned, axis=0, keepdims=True) * scale
                )

    def slot(offset):
        return pl.multiple_of((offset + 2) * TILES, TILES)

    def arrive(t, ref, sems):
        rows = pl.ds(pl.multiple_of(t * TILE, TILE), TILE)
        pltpu.make_async_copy(raw.at[rows], ref.at[rows], sems.at[t]).wait()
        left = unit_rows(ref[rows, :])
        ref[rows, :] = left
        return left

    def message(k, block, offset):
        return pltpu.make_async_remote_copy(
            src_ref=back.at[pl.ds(k * TILES, TILES)],
            dst_ref=out_ref.at[pl.ds(slot(offset), TILES)],
            send_sem=back_send_sem.at[k],
            recv_sem=back_sem.at[offset + 2],
            device_id=where_of(block),
            device_id_type=MESH,
        )

    @pl.when(has_far)
    def _():
        each_tile(
            lambda t: pair_tile(
                arrive(t, far, far_sem), unit, t, out_ref, slot(2 * s), back, 0
            )
        )
        message(0, b + 2 * s, -2 * s).start()

    @pl.when(even)
    def _():
        def near_tile(t):
            left = arrive(t, near, near_sem)
            pair_tile(left, unit, t, out_ref, slot(s), back, TILES)

            @pl.when(has_far)
            def _():
                pair_tile(left, far, t, back, 2 * TILES, back, 3 * TILES)

        each_tile(near_tile)
        message(1, mate, -s).start()

        @pl.when(has_far)
        def _():
            message(2, b + 2 * s, -s).start()
            message(3, mate, s).start()

    @pl.when(cross_e)
    def _():
        def seam_tile(t):
            left = arrive(t, extra, extra_sem)
            pair_tile(left, unit, t, out_ref, slot(1), back, 4 * TILES)
            pair_tile(left, near, t, back, 5 * TILES, back, 6 * TILES)

        each_tile(seam_tile)
        message(4, over, -1).start()
        message(5, mate, 2).start()
        message(6, over, -2).start()

    @pl.when(cross_o)
    def _():
        def seam_tile(t):
            left = arrive(t, extra, extra_sem)
            pair_tile(left, near, t, back, 5 * TILES, back, 6 * TILES)

        each_tile(seam_tile)
        message(5, mate, -2).start()
        message(6, over, 2).start()

    def landed(offset):
        rows = pl.ds(slot(offset), TILES)
        pltpu.make_async_copy(
            back.at[pl.ds(0, TILES)], out_ref.at[rows], back_sem.at[offset + 2]
        ).wait()

    landed(-2 * s)

    @pl.when(jnp.logical_not(cross_e))
    def _():
        landed(-s)

    @pl.when(odd)
    def _():
        @pl.when(has_far)
        def _():
            landed(s)

    @pl.when(no_far)
    def _():
        landed(2 * s)

        @pl.when(odd)
        def _():
            landed(s)

    for send in sends:
        settle(*send)

    @pl.when(has_far)
    def _():
        message(0, b + 2 * s, -2 * s).wait_send()

    @pl.when(even)
    def _():
        message(1, mate, -s).wait_send()

        @pl.when(has_far)
        def _():
            message(2, b + 2 * s, -s).wait_send()
            message(3, mate, s).wait_send()

    @pl.when(cross_e)
    def _():
        message(4, over, -1).wait_send()

    @pl.when(cross)
    def _():
        message(5, mate, 2 * s).wait_send()
        message(6, over, 2 * s).wait_send()


def body(embeddings):
    rows, width = embeddings.shape
    block = pltpu.VMEM((rows, width), jnp.bfloat16)
    tiles_t = pl.pallas_call(
        kernel,
        name="cycle_tile_max",
        out_shape=jax.ShapeDtypeStruct((5 * TILES, rows), jnp.float32),
        in_specs=[pl.BlockSpec(memory_space=pltpu.HBM)],
        out_specs=pl.BlockSpec(memory_space=pltpu.VMEM),
        scratch_shapes=[
            block,
            block,
            block,
            block,
            block,
            pltpu.VMEM((7 * TILES, rows), jnp.float32),
            pltpu.SemaphoreType.DMA,
            pltpu.SemaphoreType.DMA((4, TILES)),
            pltpu.SemaphoreType.DMA((TILES,)),
            pltpu.SemaphoreType.DMA((TILES,)),
            pltpu.SemaphoreType.DMA((TILES,)),
            pltpu.SemaphoreType.DMA((7,)),
            pltpu.SemaphoreType.DMA((5,)),
        ],
        compiler_params=pltpu.CompilerParams(
            collective_id=0, has_side_effects=True, vmem_limit_bytes=48 * 2**20
        ),
        cost_estimate=pl.CostEstimate(
            flops=8 * 1024**3, bytes_accessed=4 * 2**20, transcendentals=0
        ),
    )(embeddings)
    return jnp.transpose(tiles_t)


def solution(mesh):
    return jax.shard_map(
        body,
        mesh=mesh,
        in_specs=(P(("blk", "grp"), None),),
        out_specs=P(("blk", "grp"), None),
        check_vma=False,
    )
```

time: 105 us -> 75 us (0.71)
  Pallas kernels: 0 us -> 71.8 us
  waiting for transfers between devices: 52.7 us -> 0 us
  other arithmetic: 14.2 us -> 0 us
  matrix products: 12.2 us -> 0 us
  starting transfers between devices: 11.4 us -> 0 us
  local copies, waits for them, and re-layouts: 12.9 us -> 2.26 us
    pallas_call x0 -> x1, Pallas kernels: none -> 71.8 us  [body(): pl.pallas_call(kernel, name='cycle_tile_max', out_shape=jax.ShapeDtypeStr...]
    ppermute x4 -> x0, waiting for transfers between devices: 52.7 us -> none  [from_behind(): return lax.ppermute(block, axis, route)]
    dot_general x3 -> x0, matrix products: 12.2 us -> none  [score(): lax.dot_general(unit, keys, (((1,), (1,)), ((), ())), preferred_element_t...]
    ppermute x4 -> x0, starting transfers between devices: 11.4 us -> none  [from_behind(): return lax.ppermute(block, axis, route)]
    reduce_max x3 -> x0, other arithmetic: 10.1 us -> none  [tile_rows(): return jnp.max(scores.reshape(count, count // 128, 128), axis=-1)]
    unnamed x9 -> x3, local copies, waits for them, and re-layouts: 11.8 us -> 2.26 us
    reduce_sum x1 -> x0, other arithmetic: 2.07 us -> none  [body(): jnp.mean(values * values, axis=-1, keepdims=True) + 1e-06]
    convert_element_type x1 -> x0, other arithmetic: 2 us -> none  [body(): (values * lax.rsqrt(jnp.mean(values * values, axis=-1, keepdims=True) + 1...]
  transfers between devices with their start and end apart: 4 -> 0, of which waited for: 3 -> 0; matrix products, arithmetic and copies ran while one was open for 33% -> 0% of each run, Pallas kernels for 0% -> 0%
where the time goes in v1:
time: 75 us; the launch traced here: 74.1 us
  Pallas kernels  71.8 us (96%)
  local copies, waits for them, and re-layouts  2.26 us (3%)
    pallas_call x1, Pallas kernels, body(): pl.pallas_call(kernel, name='cycle_tile_max', out_shape=jax.ShapeDtypeStr...  71.8 us
    unnamed x3, local copies, waits for them, and re-layouts  2.26 us

profile of v1, /device:TPU:16, one launch (start us, length us, event | category | flops | bytes accessed | tf_op | source)
XLA Modules:
  0.0 74.1 jit_solution(3400587769452239253)
XLA Ops:
  0.0 0.0 copy-start
  0.0 1.6 %copy-done = bf16[1024,1024]{1,0:T(8,128)(2,1)S(1)} copy-done((bf16[1024,1024]{1,0:T(8,128)(2,1)S(1)}, bf16[1024,1024]{1,0:T(8,128)(2,1)}, u32[]{:S(2)}) %copy-start) | copy-done | bytes 2097176
  1.6 71.8 %cycle_tile_max.1 = f32[40,1024]{1,0:T(8,128)S(1)} custom-call(bf16[1024,1024]{1,0:T(8,128)(2,1)S(1)} %copy-done), custom_call_target="tpu_custom_call" | custom-call | flops 8589934592 | bytes 4194304 | tf_op jit(solution)/shard_map/cycle_tile_max/pallas_call | solution.py:297
  73.4 0.7 copy.3
Async XLA Ops:
  0.0 1.6 %copy-start = (bf16[1024,1024]{1,0:T(8,128)(2,1)S(1)}, bf16[1024,1024]{1,0:T(8,128)(2,1)}, u32[]{:S(2)}) copy-start(bf16[1024,1024]{1,0:T(8,128)(2,1)} %x_ref.1) | copy-start | bytes 6291460

commit v2 on v1

v2 whole, which is shorter than its diff:
```python
import jax
import jax.numpy as jnp
from jax import lax
from jax.experimental import pallas as pl
from jax.experimental.pallas import tpu as pltpu
from jax.sharding import PartitionSpec as P

MESH = pl.DeviceIdType.MESH
ROWS = 1024
TILE = 128
TILES = ROWS // TILE
UNIT = 256
UNITS = ROWS // UNIT
PIECE = 64
PIECES = ROWS // PIECE
AROUND = 5
SEAM_AROUND = 10
GRP = 2
BLOCKS = 256


def where_of(block):
    block = lax.rem(block + BLOCKS, BLOCKS)
    return (lax.div(block, GRP), lax.rem(block, GRP))


def both(*conditions):
    out = conditions[0]
    for condition in conditions[1:]:
        out = jnp.logical_and(out, condition)
    return out


def kernel(
    x_ref,
    out_ref,
    raw,
    unit,
    near,
    far,
    extra,
    pass_on,
    ring,
    back,
    load_sem,
    near_send,
    near_sem,
    ring_send,
    ring_sem,
    far_send,
    far_sem,
    extra_send,
    extra_sem,
    pass_sem,
    pass_send,
    back_send,
    back_sem,
    hello,
):
    b = lax.axis_index("blk") * GRP + lax.axis_index("grp")
    m = lax.rem(b, 4)
    z = lax.rem(lax.div(b, 4), 8)
    x = lax.rem(lax.div(b, 32), 4)
    half = lax.div(b, 128)
    y = half * 2 + lax.rem(b, 2)
    scale = 1.0 / 1024**0.5

    def at_y(offset):
        to = lax.rem(y + offset + 4, 4)
        return lax.div(to, 2) * 128 + lax.rem(b, 128) - lax.rem(b, 2) + lax.rem(to, 2)

    is_e = x >= 1
    s = jnp.where(is_e, -1, 1)
    role = jnp.where(is_e, 3 - m, m)
    even = lax.rem(role, 2) == 0
    odd = jnp.logical_not(even)
    low = m < 2
    high = jnp.logical_not(low)
    first_o = both(x == 0, z == 0)
    last_o = both(x == 0, z == 7)
    last_e = both(x == 3, z == 7)

    mate = b + 1 - 2 * lax.rem(m, 2)
    ahead = at_y(s)
    behind = at_y(-s)
    no_far = both(last_o, high)
    has_far = jnp.logical_not(no_far)
    no_send = jnp.logical_or(both(first_o, low), both(last_e, high))
    sends_far = jnp.logical_not(no_send)
    cross_e = both(last_e, m == 3)
    cross_o = both(first_o, m == 0)
    cross = jnp.logical_or(cross_e, cross_o)
    pass_e = both(last_e, m == 2)
    pass_o = both(first_o, m == 1)
    passes = jnp.logical_or(pass_e, pass_o)
    over = jnp.where(is_e, b + 1, b - 1)
    seam_e = half * 128 + 127
    seam_o = half * 128
    slow = both(last_e, low)
    around = jnp.where(last_e, jnp.where(low, SEAM_AROUND, 0), AROUND)
    direct = PIECES - around

    load = pltpu.make_async_copy(x_ref, raw, load_sem)
    load.start()

    barrier = pltpu.get_barrier_semaphore()

    def greet(condition, *blocks):
        def send():
            for block in blocks:
                pl.semaphore_signal(
                    barrier, inc=1, device_id=where_of(block), device_id_type=MESH
                )

        if condition is None:
            send()
        else:
            pl.when(condition)(send)

    greet(None, behind)
    greet(even, mate)
    greet(has_far, b + 2 * s)
    greet(cross_o, half * 128 + 126, over)
    greet(pass_o, seam_e, at_y(1))
    greet(pass_e, at_y(-1))

    def one(condition):
        return condition.astype(jnp.int32)

    pl.semaphore_wait(
        barrier,
        1
        + one(odd)
        + one(sends_far)
        + one(no_far)
        + 3 * one(cross_e)
        + one(pass_e)
        + one(cross_o),
    )

    @pl.when(cross_e)
    def _():
        for block in (over, seam_o + 1):
            pl.semaphore_signal(hello, inc=1, device_id=where_of(block), device_id_type=MESH)

    load.wait()

    def tile_rows(t, size):
        return pl.ds(pl.multiple_of(t * size, size), size)

    def around_piece(i):
        usual = jnp.where(i == 0, 7, jnp.where(i < 3, i + 9, i + 11))
        return jnp.where(slow, i, usual)

    def direct_piece(j):
        usual = jnp.where(j < 7, j, jnp.where(j < 9, j + 1, j + 3))
        return jnp.where(slow, j + SEAM_AROUND, jnp.where(last_e, j, usual))

    def remote(src, dst, send, recv, block):
        return pltpu.make_async_remote_copy(
            src_ref=src,
            dst_ref=dst,
            send_sem=send,
            recv_sem=recv,
            device_id=where_of(block),
            device_id_type=MESH,
        )

    def leg_one(i):
        p = around_piece(i)
        return remote(
            raw.at[tile_rows(p, PIECE)],
            ring.at[tile_rows(i, PIECE)],
            near_send.at[p],
            ring_sem.at[i],
            ahead,
        )

    def straight(j):
        p = direct_piece(j)
        rows = tile_rows(p, PIECE)
        return remote(raw.at[rows], near.at[rows], near_send.at[p], near_sem.at[p], mate)

    def leg_two(i):
        rows = tile_rows(i, PIECE)
        return remote(ring.at[rows], ring.at[rows], ring_send.at[i], ring_sem.at[i], ahead)

    def leg_three(i):
        p = around_piece(i)
        return remote(
            ring.at[tile_rows(i, PIECE)],
            near.at[tile_rows(p, PIECE)],
            ring_send.at[i],
            near_sem.at[p],
            ahead,
        )

    def far_copy(which, t, block):
        rows = tile_rows(t, TILE)
        return remote(raw.at[rows], far.at[rows], far_send.at[which, t], far_sem.at[t], block)

    def seam_copy(t, block):
        rows = tile_rows(t, TILE)
        return remote(raw.at[rows], pass_on.at[rows], extra_send.at[t], pass_sem.at[t], block)

    def seam_pass(t, block):
        rows = tile_rows(t, TILE)
        return remote(pass_on.at[rows], extra.at[rows], pass_send.at[t], extra_sem.at[t], block)

    def each(count, body):
        def step(t, carry):
            body(t)
            return carry

        lax.fori_loop(0, count, step, 0)

    seam_to = jnp.where(cross_e, at_y(1), at_y(-1))
    pass_to = jnp.where(pass_e, seam_o, seam_e)

    @pl.when(odd)
    def _():
        each(around, lambda i: leg_one(i).start())

        @pl.when(jnp.logical_not(slow))
        def _():
            each(direct, lambda j: straight(j).start())

    @pl.when(sends_far)
    def _():
        each(TILES, lambda t: far_copy(0, t, b - 2 * s).start())

    @pl.when(no_far)
    def _():
        each(TILES, lambda t: far_copy(1, t, b + 2 * s).start())

    @pl.when(cross)
    def _():
        each(TILES, lambda t: seam_copy(t, seam_to).start())

    def normalise(src, dst, u):
        def step(k, carry):
            rows = pl.ds(pl.multiple_of(u * UNIT + k * 32, 32), 32)
            values = src[rows, :].astype(jnp.float32)
            mean = jnp.mean(values * values, axis=-1, keepdims=True)
            dst[rows, :] = (values * lax.rsqrt(mean + 1e-06)).astype(jnp.bfloat16)
            return carry

        lax.fori_loop(0, UNIT // 32, step, 0)

    each(UNITS, lambda u: normalise(raw, unit, u))

    def scores(left, right):
        return lax.dot_general(
            left, right, (((1,), (1,)), ((), ())), preferred_element_type=jnp.float32
        )

    def own_unit(u):
        left = unit[tile_rows(u, UNIT), :]
        for n in range(UNITS):
            span = slice(n * UNIT, n * UNIT + UNIT)
            block = scores(left, unit[span, :])
            at = lax.broadcasted_iota(jnp.int32, (UNIT, UNIT), 0) + u * UNIT
            to = lax.broadcasted_iota(jnp.int32, (UNIT, UNIT), 1) + n * UNIT
            block = jnp.where(at == to, -jnp.inf, block)
            for q in range(UNIT // TILE):
                out_ref[pl.ds(16 + 2 * u + q, 1), span] = (
                    jnp.max(block[q * TILE : q * TILE + TILE, :], axis=0, keepdims=True) * scale
                )

    def pair_unit(keys_ref, rows_ref, u, by_row, row_base, by_key, key_base):
        left = keys_ref[tile_rows(u, UNIT), :]
        for n in range(UNITS):
            span = slice(n * UNIT, n * UNIT + UNIT)
            block = scores(left, rows_ref[span, :])
            for q in range(UNIT // TILE):
                part = block[q * TILE : q * TILE + TILE, :]
                by_row[pl.ds(row_base + 2 * u + q, 1), span] = (
                    jnp.max(part, axis=0, keepdims=True) * scale
                )
                columns = pl.ds(pl.multiple_of(u * UNIT + q * TILE, TILE), TILE)
                for h in range(UNIT // TILE):
                    turned = jnp.transpose(part[:, h * TILE : h * TILE + TILE])
                    by_key[pl.ds(key_base + 2 * n + h, 1), columns] = (
                        jnp.max(turned, axis=0, keepdims=True) * scale
                    )

    def slot(offset):
        return pl.multiple_of((offset + 2) * TILES, TILES)

    def take(ref, sems, u, size):
        for k in range(UNIT // size):
            t = u * (UNIT // size) + k
            rows = tile_rows(t, size)
            pltpu.make_async_copy(raw.at[rows], ref.at[rows], sems.at[t]).wait()
        normalise(ref, ref, u)

    def message(k, block, offset):
        return remote(
            back.at[pl.ds(k * TILES, TILES)],
            out_ref.at[pl.ds(slot(offset), TILES)],
            back_send.at[k],
            back_sem.at[offset + 2],
            block,
        )

    def far_unit(u):
        take(far, far_sem, u, TILE)
        pair_unit(far, unit, u, out_ref, slot(2 * s), back, 0)

    def near_unit(u):
        take(near, near_sem, u, PIECE)
        pair_unit(near, unit, u, out_ref, slot(s), back, TILES)

    def near_far_unit(u):
        pair_unit(near, far, u, back, 2 * TILES, back, 3 * TILES)

    def step(i):
        @pl.when(i < around)
        def _():
            rows = tile_rows(i, PIECE)
            pltpu.make_async_copy(raw.at[rows], ring.at[rows], ring_sem.at[i]).wait()

            @pl.when(even)
            def _():
                leg_two(i).start()

            @pl.when(odd)
            def _():
                leg_three(i).start()

        @pl.when(both(passes, i < TILES))
        def _():
            @pl.when(both(pass_o, i == 0))
            def _():
                pl.semaphore_wait(hello, 1)

            rows = tile_rows(i, TILE)
            pltpu.make_async_copy(raw.at[rows], pass_on.at[rows], pass_sem.at[i]).wait()
            seam_pass(i, pass_to).start()

        @pl.when(i < UNITS)
        def _():
            own_unit(i)

        turn = both(lax.rem(i, 2) == 1, i < 2 * UNITS)

        @pl.when(both(has_far, turn))
        def _():
            far_unit(lax.div(i, 2))

        @pl.when(both(even, jnp.logical_not(slow), jnp.logical_or(i == 4, i == 8)))
        def _():
            near_unit(lax.div(i, 4) - 1)

        @pl.when(both(cross_e, lax.rem(i, 2) == 0, i >= 2))
        def _():
            u = lax.div(i, 2) - 1
            take(extra, extra_sem, u, TILE)
            pair_unit(extra, unit, u, out_ref, slot(1), back, 4 * TILES)

    each(10, step)

    @pl.when(slow)
    def _():
        @pl.when(odd)
        def _():
            each(direct, lambda j: straight(j).start())

    @pl.when(has_far)
    def _():
        message(0, b + 2 * s, -2 * s).start()

    @pl.when(cross_e)
    def _():
        message(4, over, -1).start()
        near_unit(2)
        near_unit(3)
        each(UNITS, lambda u: pair_unit(extra, near, u, back, 5 * TILES, back, 6 * TILES))
        message(5, mate, 2).start()
        message(6, over, -2).start()
        each(UNITS, near_far_unit)

    @pl.when(both(even, jnp.logical_not(cross_e)))
    def _():
        done = jnp.where(slow, 0, 2)

        @pl.when(has_far)
        def _():
            each(done, near_far_unit)

        def rest(k):
            near_unit(done + k)

            @pl.when(has_far)
            def _():
                near_far_unit(done + k)

        each(UNITS - done, rest)

    @pl.when(even)
    def _():
        message(1, mate, -s).start()

        @pl.when(has_far)
        def _():
            message(2, b + 2 * s, -s).start()
            message(3, mate, s).start()

    @pl.when(cross_o)
    def _():
        def seam_unit(u):
            take(extra, extra_sem, u, TILE)
            pair_unit(extra, near, u, back, 5 * TILES, back, 6 * TILES)

        each(UNITS, seam_unit)
        message(5, mate, -2).start()
        pl.semaphore_wait(hello, 1)
        message(6, over, 2).start()

    def landed(offset):
        pltpu.make_async_copy(
            back.at[pl.ds(0, TILES)],
            out_ref.at[pl.ds(slot(offset), TILES)],
            back_sem.at[offset + 2],
        ).wait()

    landed(-2 * s)

    @pl.when(jnp.logical_not(cross_e))
    def _():
        landed(-s)

    @pl.when(odd)
    def _():
        landed(s)

    @pl.when(no_far)
    def _():
        landed(2 * s)

    @pl.when(odd)
    def _():
        each(around, lambda i: leg_one(i).wait_send())
        each(direct, lambda j: straight(j).wait_send())
        each(around, lambda i: leg_three(i).wait_send())

    @pl.when(even)
    def _():
        each(around, lambda i: leg_two(i).wait_send())

    @pl.when(sends_far)
    def _():
        each(TILES, lambda t: far_copy(0, t, b - 2 * s).wait_send())

    @pl.when(no_far)
    def _():
        each(TILES, lambda t: far_copy(1, t, b + 2 * s).wait_send())

    @pl.when(cross)
    def _():
        each(TILES, lambda t: seam_copy(t, seam_to).wait_send())

    @pl.when(passes)
    def _():
        each(TILES, lambda t: seam_pass(t, pass_to).wait_send())

    @pl.when(has_far)
    def _():
        message(0, b + 2 * s, -2 * s).wait_send()

    @pl.when(even)
    def _():
        message(1, mate, -s).wait_send()

        @pl.when(has_far)
        def _():
            message(2, b + 2 * s, -s).wait_send()
            message(3, mate, s).wait_send()

    @pl.when(cross_e)
    def _():
        message(4, over, -1).wait_send()

    @pl.when(cross)
    def _():
        message(5, mate, 2 * s).wait_send()
        message(6, over, 2 * s).wait_send()


def body(embeddings):
    rows, width = embeddings.shape
    block = pltpu.VMEM((rows, width), jnp.bfloat16)
    dma = pltpu.SemaphoreType.DMA
    tiles_t = pl.pallas_call(
        kernel,
        name="cycle_tile_max",
        out_shape=jax.ShapeDtypeStruct((5 * TILES, rows), jnp.float32),
        in_specs=[pl.BlockSpec(memory_space=pltpu.HBM)],
        out_specs=pl.BlockSpec(memory_space=pltpu.VMEM),
        scratch_shapes=[
            block,
            block,
            block,
            block,
            block,
            block,
            pltpu.VMEM((SEAM_AROUND * PIECE, width), jnp.bfloat16),
            pltpu.VMEM((7 * TILES, rows), jnp.float32),
            dma,
            dma((PIECES,)),
            dma((PIECES,)),
            dma((SEAM_AROUND,)),
            dma((SEAM_AROUND,)),
            dma((2, TILES)),
            dma((TILES,)),
            dma((TILES,)),
            dma((TILES,)),
            dma((TILES,)),
            dma((TILES,)),
            dma((7,)),
            dma((5,)),
            pltpu.SemaphoreType.REGULAR,
        ],
        compiler_params=pltpu.CompilerParams(
            collective_id=0, has_side_effects=True, vmem_limit_bytes=62 * 2**20 + 2**18
        ),
        cost_estimate=pl.CostEstimate(
            flops=8 * 1024**3, bytes_accessed=4 * 2**20, transcendentals=0
        ),
    )(embeddings)
    return jnp.transpose(tiles_t)


def solution(mesh):
    return jax.shard_map(
        body,
        mesh=mesh,
        in_specs=(P(("blk", "grp"), None),),
        out_specs=P(("blk", "grp"), None),
        check_vma=False,
    )
```

time: 75 us -> 56.5 us (0.75); the launches traced: 74.1 us -> 56.4 us
  Pallas kernels: 71.8 us -> 54.8 us
    pallas_call x1, Pallas kernels: 71.8 us -> 54.8 us  [body(): pl.pallas_call(kernel, name='cycle_tile_max', out_shape=jax.ShapeDtypeStr...]
    unnamed x3 -> x1, local copies, waits for them, and re-layouts: 2.26 us -> 1.59 us
where the time goes in v2:
time: 56.5 us; the launch traced here: 56.4 us
  Pallas kernels  54.8 us (97%)
  local copies, waits for them, and re-layouts  1.59 us (3%)
    pallas_call x1, Pallas kernels, body(): pl.pallas_call(kernel, name='cycle_tile_max', out_shape=jax.ShapeDtypeStr...  54.8 us
    unnamed x1, local copies, waits for them, and re-layouts  1.59 us

profile of v2, /device:TPU:16, one launch (start us, length us, event | category | flops | bytes accessed | tf_op | source)
XLA Modules:
  0.0 56.4 jit_solution(11074941514347567534)
XLA Ops:
  0.0 54.8 %cycle_tile_max.1 = f32[40,1024]{1,0:T(8,128)} custom-call(bf16[1024,1024]{1,0:T(8,128)(2,1)} %x_ref.1), custom_call_target="tpu_custom_call" | custom-call | flops 8589934592 | bytes 4194304 | tf_op jit(solution)/shard_map/cycle_tile_max/pallas_call | solution.py:494
  54.8 1.6 %copy.3 = f32[1024,40]{0,1:T(8,128)} copy(f32[1024,40]{0,1:T(8,128)} %bitcast.1) | data formatting | bytes 327680

commit v3 on v2

--- a/solution.py
+++ b/solution.py
@@ -127,23 +127,25 @@
     def one(condition):
         return condition.astype(jnp.int32)
 
-    pl.semaphore_wait(
-        barrier,
-        1
-        + one(odd)
-        + one(sends_far)
-        + one(no_far)
-        + 3 * one(cross_e)
-        + one(pass_e)
-        + one(cross_o),
-    )
+    with jax.named_scope("bar"):
+        pl.semaphore_wait(
+            barrier,
+            1
+            + one(odd)
+            + one(sends_far)
+            + one(no_far)
+            + 3 * one(cross_e)
+            + one(pass_e)
+            + one(cross_o),
+        )
 
     @pl.when(cross_e)
     def _():
         for block in (over, seam_o + 1):
             pl.semaphore_signal(hello, inc=1, device_id=where_of(block), device_id_type=MESH)
 
-    load.wait()
+    with jax.named_scope("load"):
+        load.wait()
 
     def tile_rows(t, size):
         return pl.ds(pl.multiple_of(t * size, size), size)
@@ -200,11 +202,11 @@
         return remote(raw.at[rows], far.at[rows], far_send.at[which, t], far_sem.at[t], block)
 
     def seam_copy(t, block):
-        rows = tile_rows(t, TILE)
+        rows = tile_rows(t, PIECE)
         return remote(raw.at[rows], pass_on.at[rows], extra_send.at[t], pass_sem.at[t], block)
 
     def seam_pass(t, block):
-        rows = tile_rows(t, TILE)
+        rows = tile_rows(t, PIECE)
         return remote(pass_on.at[rows], extra.at[rows], pass_send.at[t], extra_sem.at[t], block)
 
     def each(count, body):
@@ -235,19 +237,17 @@
 
     @pl.when(cross)
     def _():
-        each(TILES, lambda t: seam_copy(t, seam_to).start())
+        each(PIECES, lambda t: seam_copy(t, seam_to).start())
 
     def normalise(src, dst, u):
-        def step(k, carry):
-            rows = pl.ds(pl.multiple_of(u * UNIT + k * 32, 32), 32)
+        for k in range(UNIT // 64):
+            rows = pl.ds(pl.multiple_of(u * UNIT + k * 64, 64), 64)
             values = src[rows, :].astype(jnp.float32)
             mean = jnp.mean(values * values, axis=-1, keepdims=True)
             dst[rows, :] = (values * lax.rsqrt(mean + 1e-06)).astype(jnp.bfloat16)
-            return carry
-
-        lax.fori_loop(0, UNIT // 32, step, 0)
-
-    each(UNITS, lambda u: normalise(raw, unit, u))
+
+    with jax.named_scope("norm"):
+        each(UNITS, lambda u: normalise(raw, unit, u))
 
     def scores(left, right):
         return lax.dot_general(
@@ -304,21 +304,51 @@
         )
 
     def far_unit(u):
-        take(far, far_sem, u, TILE)
-        pair_unit(far, unit, u, out_ref, slot(2 * s), back, 0)
+        with jax.named_scope("farw"):
+            take(far, far_sem, u, TILE)
+        with jax.named_scope("farc"):
+            pair_unit(far, unit, u, out_ref, slot(2 * s), back, 0)
 
     def near_unit(u):
-        take(near, near_sem, u, PIECE)
-        pair_unit(near, unit, u, out_ref, slot(s), back, TILES)
+        with jax.named_scope("nearw"):
+            take(near, near_sem, u, PIECE)
+        with jax.named_scope("nearc"):
+            pair_unit(near, unit, u, out_ref, slot(s), back, TILES)
 
     def near_far_unit(u):
-        pair_unit(near, far, u, back, 2 * TILES, back, 3 * TILES)
-
-    def step(i):
+        with jax.named_scope("nfc"):
+            pair_unit(near, far, u, back, 2 * TILES, back, 3 * TILES)
+
+    def extra_unit(u):
+        with jax.named_scope("xw"):
+            take(extra, extra_sem, u, PIECE)
+        with jax.named_scope("xuc"):
+            pair_unit(extra, unit, u, out_ref, slot(1), back, 4 * TILES)
+
+    def extra_near_unit(u):
+        with jax.named_scope("xnc"):
+            pair_unit(extra, near, u, back, 5 * TILES, back, 6 * TILES)
+
+    def forward(i):
+        @pl.when(both(passes, i < TILES))
+        def _():
+            @pl.when(both(pass_o, i == 0))
+            def _():
+                with jax.named_scope("hello"):
+                    pl.semaphore_wait(hello, 1)
+
+            for k in range(TILE // PIECE):
+                t = i * (TILE // PIECE) + k
+                rows = tile_rows(t, PIECE)
+                with jax.named_scope("passw"):
+                    pltpu.make_async_copy(raw.at[rows], pass_on.at[rows], pass_sem.at[t]).wait()
+                seam_pass(t, pass_to).start()
+
         @pl.when(i < around)
         def _():
             rows = tile_rows(i, PIECE)
-            pltpu.make_async_copy(raw.at[rows], ring.at[rows], ring_sem.at[i]).wait()
+            with jax.named_scope("ringw"):
+                pltpu.make_async_copy(raw.at[rows], ring.at[rows], ring_sem.at[i]).wait()
 
             @pl.when(even)
             def _():
@@ -328,89 +358,83 @@
             def _():
                 leg_three(i).start()
 
-        @pl.when(both(passes, i < TILES))
-        def _():
-            @pl.when(both(pass_o, i == 0))
+        @pl.when(i < UNITS)
+        def _():
+            with jax.named_scope("own"):
+                own_unit(i)
+
+    each(jnp.where(passes, TILES, jnp.where(slow, SEAM_AROUND, AROUND)), forward)
+
+    @pl.when(both(slow, odd))
+    def _():
+        each(direct, lambda j: straight(j).start())
+
+    def arrive(k):
+        @pl.when(has_far)
+        def _():
+            far_unit(k)
+
+        @pl.when(both(even, jnp.logical_not(cross_e), jnp.logical_or(k == 1, k == 2)))
+        def _():
+            near_unit(k - 1)
+
+    each(UNITS, arrive)
+
+    @pl.when(has_far)
+    def _():
+        message(0, b + 2 * s, -2 * s).start()
+
+    @pl.when(both(even, jnp.logical_not(cross_e)))
+    def _():
+        @pl.when(has_far)
+        def _():
+            each(2, near_far_unit)
+
+        def rest(k):
+            near_unit(2 + k)
+
+            @pl.when(has_far)
             def _():
-                pl.semaphore_wait(hello, 1)
-
-            rows = tile_rows(i, TILE)
-            pltpu.make_async_copy(raw.at[rows], pass_on.at[rows], pass_sem.at[i]).wait()
-            seam_pass(i, pass_to).start()
-
-        @pl.when(i < UNITS)
-        def _():
-            own_unit(i)
-
-        turn = both(lax.rem(i, 2) == 1, i < 2 * UNITS)
-
-        @pl.when(both(has_far, turn))
-        def _():
-            far_unit(lax.div(i, 2))
-
-        @pl.when(both(even, jnp.logical_not(slow), jnp.logical_or(i == 4, i == 8)))
-        def _():
-            near_unit(lax.div(i, 4) - 1)
-
-        @pl.when(both(cross_e, lax.rem(i, 2) == 0, i >= 2))
-        def _():
-            u = lax.div(i, 2) - 1
-            take(extra, extra_sem, u, TILE)
-            pair_unit(extra, unit, u, out_ref, slot(1), back, 4 * TILES)
-
-    each(10, step)
-
-    @pl.when(slow)
-    def _():
-        @pl.when(odd)
-        def _():
-            each(direct, lambda j: straight(j).start())
-
-    @pl.when(has_far)
-    def _():
-        message(0, b + 2 * s, -2 * s).start()
+                near_far_unit(2 + k)
+
+        each(2, rest)
 
     @pl.when(cross_e)
     def _():
+        def all_four(u):
+            near_unit(u)
+            near_far_unit(u)
+
+            @pl.when(u < UNITS - 1)
+            def _():
+                extra_unit(u)
+
+        each(UNITS, all_four)
+
+    @pl.when(even)
+    def _():
+        message(1, mate, -s).start()
+
+        @pl.when(has_far)
+        def _():
+            message(2, b + 2 * s, -s).start()
+            message(3, mate, s).start()
+
+    @pl.when(cross_e)
+    def _():
+        each(UNITS - 1, extra_near_unit)
+        extra_unit(UNITS - 1)
         message(4, over, -1).start()
-        near_unit(2)
-        near_unit(3)
-        each(UNITS, lambda u: pair_unit(extra, near, u, back, 5 * TILES, back, 6 * TILES))
+        extra_near_unit(UNITS - 1)
         message(5, mate, 2).start()
         message(6, over, -2).start()
-        each(UNITS, near_far_unit)
-
-    @pl.when(both(even, jnp.logical_not(cross_e)))
-    def _():
-        done = jnp.where(slow, 0, 2)
-
-        @pl.when(has_far)
-        def _():
-            each(done, near_far_unit)
-
-        def rest(k):
-            near_unit(done + k)
-
-            @pl.when(has_far)
-            def _():
-                near_far_unit(done + k)
-
-        each(UNITS - done, rest)
-
-    @pl.when(even)
-    def _():
-        message(1, mate, -s).start()
-
-        @pl.when(has_far)
-        def _():
-            message(2, b + 2 * s, -s).start()
-            message(3, mate, s).start()
 
     @pl.when(cross_o)
     def _():
         def seam_unit(u):
-            take(extra, extra_sem, u, TILE)
-            pair_unit(extra, near, u, back, 5 * TILES, back, 6 * TILES)
+            with jax.named_scope("xw"):
+                take(extra, extra_sem, u, PIECE)
+            extra_near_unit(u)
 
         each(UNITS, seam_unit)
         message(5, mate, -2).start()
@@ -424,67 +448,69 @@
             back_sem.at[offset + 2],
         ).wait()
 
-    landed(-2 * s)
-
-    @pl.when(jnp.logical_not(cross_e))
-    def _():
-        landed(-s)
-
-    @pl.when(odd)
-    def _():
-        landed(s)
-
-    @pl.when(no_far)
-    def _():
-        landed(2 * s)
-
-    @pl.when(odd)
-    def _():
-        each(around, lambda i: leg_one(i).wait_send())
-        each(direct, lambda j: straight(j).wait_send())
-        each(around, lambda i: leg_three(i).wait_send())
-
-    @pl.when(even)
-    def _():
-        each(around, lambda i: leg_two(i).wait_send())
-
-    @pl.when(sends_far)
-    def _():
-        each(TILES, lambda t: far_copy(0, t, b - 2 * s).wait_send())
-
-    @pl.when(no_far)
-    def _():
-        each(TILES, lambda t: far_copy(1, t, b + 2 * s).wait_send())
-
-    @pl.when(cross)
-    def _():
-        each(TILES, lambda t: seam_copy(t, seam_to).wait_send())
-
-    @pl.when(passes)
-    def _():
-        each(TILES, lambda t: seam_pass(t, pass_to).wait_send())
-
-    @pl.when(has_far)
-    def _():
-        message(0, b + 2 * s, -2 * s).wait_send()
-
-    @pl.when(even)
-    def _():
-        message(1, mate, -s).wait_send()
+    with jax.named_scope("landed"):
+        landed(-2 * s)
+
+        @pl.when(jnp.logical_not(cross_e))
+        def _():
+            landed(-s)
+
+        @pl.when(odd)
+        def _():
+            landed(s)
+
+        @pl.when(no_far)
+        def _():
+            landed(2 * s)
+
+    with jax.named_scope("settle"):
+        @pl.when(odd)
+        def _():
+            each(around, lambda i: leg_one(i).wait_send())
+            each(direct, lambda j: straight(j).wait_send())
+            each(around, lambda i: leg_three(i).wait_send())
+
+        @pl.when(even)
+        def _():
+            each(around, lambda i: leg_two(i).wait_send())
+
+        @pl.when(sends_far)
+        def _():
+            each(TILES, lambda t: far_copy(0, t, b - 2 * s).wait_send())
+
+        @pl.when(no_far)
+        def _():
+            each(TILES, lambda t: far_copy(1, t, b + 2 * s).wait_send())
+
+        @pl.when(cross)
+        def _():
+            each(PIECES, lambda t: seam_copy(t, seam_to).wait_send())
+
+        @pl.when(passes)
+        def _():
+            each(PIECES, lambda t: seam_pass(t, pass_to).wait_send())
 
         @pl.when(has_far)
         def _():
-            message(2, b + 2 * s, -s).wait_send()
-            message(3, mate, s).wait_send()
-
-    @pl.when(cross_e)
-    def _():
-        message(4, over, -1).wait_send()
-
-    @pl.when(cross)
-    def _():
-        message(5, mate, 2 * s).wait_send()
-        message(6, over, 2 * s).wait_send()
+            message(0, b + 2 * s, -2 * s).wait_send()
+
+        @pl.when(even)
+        def _():
+            message(1, mate, -s).wait_send()
+
+            @pl.when(has_far)
+            def _():
+                message(2, b + 2 * s, -s).wait_send()
+                message(3, mate, s).wait_send()
+
+        @pl.when(cross_e)
+        def _():
+            message(4, over, -1).wait_send()
+
+        @pl.when(cross)
+        def _():
+            message(5, mate, 2 * s).wait_send()
+            message(6, over, 2 * s).wait_send()
 
 
 def body(embeddings):
@@ -513,16 +539,16 @@
             dma((SEAM_AROUND,)),
             dma((2, TILES)),
             dma((TILES,)),
-            dma((TILES,)),
-            dma((TILES,)),
-            dma((TILES,)),
-            dma((TILES,)),
+            dma((PIECES,)),
+            dma((PIECES,)),
+            dma((PIECES,)),
+            dma((PIECES,)),
             dma((7,)),
             dma((5,)),
             pltpu.SemaphoreType.REGULAR,
         ],
         compiler_params=pltpu.CompilerParams(
-            collective_id=0, has_side_effects=True, vmem_limit_bytes=62 * 2**20 + 2**18
+            collective_id=0, has_side_effects=True, vmem_limit_bytes=52 * 2**20
         ),
         cost_estimate=pl.CostEstimate(
             flops=8 * 1024**3, bytes_accessed=4 * 2**20, transcendentals=0

time: 56.5 us -> 47 us (0.83)
  Pallas kernels: 54.8 us -> 45.7 us
  local copies, waits for them, and re-layouts: 1.59 us -> 0.67 us
    pallas_call x1, Pallas kernels: 54.8 us -> 45.7 us  [body(): pl.pallas_call(kernel, name='cycle_tile_max', out_shape=jax.ShapeDtypeStr...]
    unnamed x1, local copies, waits for them, and re-layouts: 1.59 us -> 0.67 us
where the time goes in v3:
time: 47 us; the launch traced here: 46.4 us
  Pallas kernels  45.7 us (97%)
  local copies, waits for them, and re-layouts  0.67 us (1%)
    pallas_call x1, Pallas kernels, body(): pl.pallas_call(kernel, name='cycle_tile_max', out_shape=jax.ShapeDtypeStr...  45.7 us

profile of v3, /device:TPU:16, one launch (start us, length us, event | category | flops | bytes accessed | tf_op | source)
XLA Modules:
  0.0 46.4 jit_solution(16857873780507610382)
XLA Ops:
  0.0 45.7 %cycle_tile_max.1 = f32[40,1024]{1,0:T(8,128)S(1)} custom-call(bf16[1024,1024]{1,0:T(8,128)(2,1)} %x_ref.1), custom_call_target="tpu_custom_call" | custom-call | flops 8589934592 | bytes 4194304 | tf_op jit(solution)/shard_map/cycle_tile_max/pallas_call | solution.py:520
  45.7 0.7 %copy.3 = f32[1024,40]{0,1:T(8,128)} copy(f32[1024,40]{0,1:T(8,128)S(1)} %bitcast.1) | data formatting | bytes 327680

commit v4 on v3

--- a/solution.py
+++ b/solution.py
@@ -15,6 +15,7 @@
 PIECES = ROWS // PIECE
 AROUND = 5
 SEAM_AROUND = 10
+LEAD = 4
 GRP = 2
 BLOCKS = 256
 
@@ -39,6 +40,9 @@
     near,
     far,
     extra,
+    near_in,
+    far_in,
+    extra_in,
     pass_on,
     ring,
     back,
@@ -56,6 +60,7 @@
     back_send,
     back_sem,
     hello,
+    far_hello,
 ):
     b = lax.axis_index("blk") * GRP + lax.axis_index("grp")
     m = lax.rem(b, 4)
@@ -97,6 +102,10 @@
     seam_e = half * 128 + 127
     seam_o = half * 128
     slow = both(last_e, low)
+    step_in = both(is_e, z == 0, low)
+    step_out = both(is_e, z == 7, high)
+    answers = both(is_e, jnp.logical_not(step_in))
+    asks = both(is_e, sends_far, jnp.logical_not(step_out))
     around = jnp.where(last_e, jnp.where(low, SEAM_AROUND, 0), AROUND)
     direct = PIECES - around
 
@@ -119,7 +128,8 @@
 
     greet(None, behind)
     greet(even, mate)
-    greet(has_far, b + 2 * s)
+    greet(both(has_far, jnp.logical_not(answers)), b + 2 * s)
+    greet(asks, b - 2 * s)
     greet(cross_o, half * 128 + 126, over)
     greet(pass_o, seam_e, at_y(1))
     greet(pass_e, at_y(-1))
@@ -132,7 +142,8 @@
             barrier,
             1
             + one(odd)
-            + one(sends_far)
+            + one(both(sends_far, jnp.logical_not(asks)))
+        + one(answers)
             + one(no_far)
             + 3 * one(cross_e)
             + one(pass_e)
@@ -143,6 +154,12 @@
     def _():
         for block in (over, seam_o + 1):
             pl.semaphore_signal(hello, inc=1, device_id=where_of(block), device_id_type=MESH)
+
+    @pl.when(answers)
+    def _():
+        pl.semaphore_signal(
+            far_hello, inc=1, device_id=where_of(b + 2 * s), device_id_type=MESH
+        )
 
     with jax.named_scope("load"):
         load.wait()
@@ -181,7 +198,7 @@
     def straight(j):
         p = direct_piece(j)
         rows = tile_rows(p, PIECE)
-        return remote(raw.at[rows], near.at[rows], near_send.at[p], near_sem.at[p], mate)
+        return remote(raw.at[rows], near_in.at[rows], near_send.at[p], near_sem.at[p], mate)
 
     def leg_two(i):
         rows = tile_rows(i, PIECE)
@@ -191,7 +208,7 @@
         p = around_piece(i)
         return remote(
             ring.at[tile_rows(i, PIECE)],
-            near.at[tile_rows(p, PIECE)],
+            near_in.at[tile_rows(p, PIECE)],
             ring_send.at[i],
             near_sem.at[p],
             ahead,
@@ -199,7 +216,7 @@
 
     def far_copy(which, t, block):
         rows = tile_rows(t, TILE)
-        return remote(raw.at[rows], far.at[rows], far_send.at[which, t], far_sem.at[t], block)
+        return remote(raw.at[rows], far_in.at[rows], far_send.at[which, t], far_sem.at[t], block)
 
     def seam_copy(t, block):
         rows = tile_rows(t, PIECE)
@@ -207,7 +224,7 @@
 
     def seam_pass(t, block):
         rows = tile_rows(t, PIECE)
-        return remote(pass_on.at[rows], extra.at[rows], pass_send.at[t], extra_sem.at[t], block)
+        return remote(pass_on.at[rows], extra_in.at[rows], pass_send.at[t], extra_sem.at[t], block)
 
     def each(count, body):
         def step(t, carry):
@@ -226,14 +243,6 @@
         @pl.when(jnp.logical_not(slow))
         def _():
             each(direct, lambda j: straight(j).start())
-
-    @pl.when(sends_far)
-    def _():
-        each(TILES, lambda t: far_copy(0, t, b - 2 * s).start())
-
-    @pl.when(no_far)
-    def _():
-        each(TILES, lambda t: far_copy(1, t, b + 2 * s).start())
 
     @pl.when(cross)
     def _():
@@ -248,6 +257,19 @@
 
     with jax.named_scope("norm"):
         each(UNITS, lambda u: normalise(raw, unit, u))
+
+    @pl.when(asks)
+    def _():
+        with jax.named_scope("fhello"):
+            pl.semaphore_wait(far_hello, 1)
+
+    @pl.when(sends_far)
+    def _():
+        each(TILES, lambda t: far_copy(0, t, b - 2 * s).start())
+
+    @pl.when(no_far)
+    def _():
+        each(TILES, lambda t: far_copy(1, t, b + 2 * s).start())
 
     def scores(left, right):
         return lax.dot_general(
@@ -287,12 +309,12 @@
     def slot(offset):
         return pl.multiple_of((offset + 2) * TILES, TILES)
 
-    def take(ref, sems, u, size):
+    def take(landing, ref, sems, u, size):
         for k in range(UNIT // size):
             t = u * (UNIT // size) + k
             rows = tile_rows(t, size)
-            pltpu.make_async_copy(raw.at[rows], ref.at[rows], sems.at[t]).wait()
-        normalise(ref, ref, u)
+            pltpu.make_async_copy(raw.at[rows], landing.at[rows], sems.at[t]).wait()
+        normalise(landing, ref, u)
 
     def message(k, block, offset):
         return remote(
@@ -305,23 +327,32 @@
 
     def far_unit(u):
         with jax.named_scope("farw"):
-            take(far, far_sem, u, TILE)
+            take(far_in, far, far_sem, u, TILE)
         with jax.named_scope("farc"):
             pair_unit(far, unit, u, out_ref, slot(2 * s), back, 0)
 
-    def near_unit(u):
+    def near_take(u):
         with jax.named_scope("nearw"):
-            take(near, near_sem, u, PIECE)
+            take(near_in, near, near_sem, u, PIECE)
+
+    def near_score(u):
         with jax.named_scope("nearc"):
             pair_unit(near, unit, u, out_ref, slot(s), back, TILES)
+
+    def near_unit(u):
+        near_take(u)
+        near_score(u)
 
     def near_far_unit(u):
         with jax.named_scope("nfc"):
             pair_unit(near, far, u, back, 2 * TILES, back, 3 * TILES)
 
+    def extra_take(u):
+        with jax.named_scope("xw"):
+            take(extra_in, extra, extra_sem, u, PIECE)
+
     def extra_unit(u):
-        with jax.named_scope("xw"):
-            take(extra, extra_sem, u, PIECE)
+        extra_take(u)
         with jax.named_scope("xuc"):
             pair_unit(extra, unit, u, out_ref, slot(1), back, 4 * TILES)
 
@@ -329,20 +360,26 @@
         with jax.named_scope("xnc"):
             pair_unit(extra, near, u, back, 5 * TILES, back, 6 * TILES)
 
+    def seam_forward(t):
+        rows = tile_rows(t, PIECE)
+        with jax.named_scope("passw"):
+            pltpu.make_async_copy(raw.at[rows], pass_on.at[rows], pass_sem.at[t]).wait()
+        seam_pass(t, pass_to).start()
+
+    @pl.when(passes)
+    def _():
+        @pl.when(pass_o)
+        def _():
+            with jax.named_scope("hello"):
+                pl.semaphore_wait(hello, 1)
+
+        each(LEAD, seam_forward)
+
     def forward(i):
-        @pl.when(both(passes, i < TILES))
-        def _():
-            @pl.when(both(pass_o, i == 0))
-            def _():
-                with jax.named_scope("hello"):
-                    pl.semaphore_wait(hello, 1)
-
-            for k in range(TILE // PIECE):
-                t = i * (TILE // PIECE) + k
-                rows = tile_rows(t, PIECE)
-                with jax.named_scope("passw"):
-                    pltpu.make_async_copy(raw.at[rows], pass_on.at[rows], pass_sem.at[t]).wait()
-                seam_pass(t, pass_to).start()
+        @pl.when(both(passes, i < (PIECES - LEAD) // 2))
+        def _():
+            seam_forward(LEAD + 2 * i)
+            seam_forward(LEAD + 2 * i + 1)
 
         @pl.when(i < around)
         def _():
@@ -358,23 +395,29 @@
             def _():
                 leg_three(i).start()
 
+        @pl.when(both(slow, odd, i == 8))
+        def _():
+            each(direct, lambda j: straight(j).start())
+
         @pl.when(i < UNITS)
         def _():
             with jax.named_scope("own"):
                 own_unit(i)
 
-    each(jnp.where(passes, TILES, jnp.where(slow, SEAM_AROUND, AROUND)), forward)
-
-    @pl.when(both(slow, odd))
-    def _():
-        each(direct, lambda j: straight(j).start())
+    each(jnp.where(passes, (PIECES - LEAD) // 2, jnp.where(slow, SEAM_AROUND, AROUND)), forward)
+
+    plain = both(even, jnp.logical_not(cross_e))
 
     def arrive(k):
+        @pl.when(both(even, step_in, k == 3))
+        def _():
+            near_unit(2)
+
         @pl.when(has_far)
         def _():
             far_unit(k)
 
-        @pl.when(both(even, jnp.logical_not(cross_e), jnp.logical_or(k == 1, k == 2)))
+        @pl.when(both(plain, jnp.logical_or(k == 1, k == 2)))
         def _():
             near_unit(k - 1)
 
@@ -384,20 +427,35 @@
     def _():
         message(0, b + 2 * s, -2 * s).start()
 
-    @pl.when(both(even, jnp.logical_not(cross_e)))
-    def _():
+    @pl.when(plain)
+    def _():
+        def rest(k):
+            @pl.when(both(k == 2, jnp.logical_not(step_in)))
+            def _():
+                near_unit(2)
+
+            @pl.when(both(cross_o, k == 2))
+            def _():
+                extra_take(0)
+                extra_take(1)
+
+            @pl.when(k == 3)
+            def _():
+                near_take(3)
+
+            @pl.when(has_far)
+            def _():
+                near_far_unit(k)
+
+        each(UNITS, rest)
+
         @pl.when(has_far)
         def _():
-            each(2, near_far_unit)
-
-        def rest(k):
-            near_unit(2 + k)
-
-            @pl.when(has_far)
-            def _():
-                near_far_unit(2 + k)
-
-        each(2, rest)
+            message(2, b + 2 * s, -s).start()
+            message(3, mate, s).start()
+
+        near_score(3)
+        message(1, mate, -s).start()
 
     @pl.when(cross_e)
     def _():
@@ -410,15 +468,9 @@
                 extra_unit(u)
 
         each(UNITS, all_four)
-
-    @pl.when(even)
-    def _():
+        message(2, b + 2 * s, -s).start()
+        message(3, mate, s).start()
         message(1, mate, -s).start()
-
-        @pl.when(has_far)
-        def _():
-            message(2, b + 2 * s, -s).start()
-            message(3, mate, s).start()
 
     @pl.when(cross_e)
     def _():
@@ -432,8 +484,10 @@
     @pl.when(cross_o)
     def _():
         def seam_unit(u):
-            with jax.named_scope("xw"):
-                take(extra, extra_sem, u, PIECE)
+            @pl.when(u >= 2)
+            def _():
+                extra_take(u)
+
             extra_near_unit(u)
 
         each(UNITS, seam_unit)
@@ -524,6 +578,9 @@
         in_specs=[pl.BlockSpec(memory_space=pltpu.HBM)],
         out_specs=pl.BlockSpec(memory_space=pltpu.VMEM),
         scratch_shapes=[
+            block,
+            block,
+            block,
             block,
             block,
             block,
@@ -546,6 +603,7 @@
             dma((7,)),
             dma((5,)),
             pltpu.SemaphoreType.REGULAR,
+            pltpu.SemaphoreType.REGULAR,
         ],
         compiler_params=pltpu.CompilerParams(
             collective_id=0, has_side_effects=True, vmem_limit_bytes=52 * 2**20

time: 47 us -> 46.5 us (0.989)
  no operation moved by 1% of the time
where the time goes in v4:
time: 46.5 us; the launch traced here: 46.4 us
  Pallas kernels  45.7 us (98%)
  local copies, waits for them, and re-layouts  0.67 us (1%)
    pallas_call x1, Pallas kernels, body(): pl.pallas_call(kernel, name='cycle_tile_max', out_shape=jax.ShapeDtypeStr...  45.7 us

profile of v4, /device:TPU:16, one launch (start us, length us, event | category | flops | bytes accessed | tf_op | source)
XLA Modules:
  0.0 46.4 jit_solution(2953789596624926023)
XLA Ops:
  0.0 45.7 %cycle_tile_max.1 = f32[40,1024]{1,0:T(8,128)S(1)} custom-call(bf16[1024,1024]{1,0:T(8,128)(2,1)} %x_ref.1), custom_call_target="tpu_custom_call" | custom-call | flops 8589934592 | bytes 4194304 | tf_op jit(solution)/shard_map/cycle_tile_max/pallas_call | solution.py:574
  45.7 0.7 %copy.3 = f32[1024,40]{0,1:T(8,128)} copy(f32[1024,40]{0,1:T(8,128)S(1)} %bitcast.1) | data formatting | bytes 327680

commit v5 on v4

--- a/solution.py
+++ b/solution.py
@@ -106,7 +106,7 @@
     step_out = both(is_e, z == 7, high)
     answers = both(is_e, jnp.logical_not(step_in))
     asks = both(is_e, sends_far, jnp.logical_not(step_out))
-    around = jnp.where(last_e, jnp.where(low, SEAM_AROUND, 0), AROUND)
+    around = jnp.where(last_e, jnp.where(low, SEAM_AROUND, 0), jnp.where(low, AROUND, AROUND + 1))
     direct = PIECES - around
 
     load = pltpu.make_async_copy(x_ref, raw, load_sem)
@@ -168,11 +168,15 @@
         return pl.ds(pl.multiple_of(t * size, size), size)
 
     def around_piece(i):
-        usual = jnp.where(i == 0, 7, jnp.where(i < 3, i + 9, i + 11))
+        five = jnp.where(i < 3, i + 9, i + 11)
+        six = jnp.where(i < 4, i + 8, i + 10)
+        usual = jnp.where(i == 0, 7, jnp.where(low, five, six))
         return jnp.where(slow, i, usual)
 
     def direct_piece(j):
-        usual = jnp.where(j < 7, j, jnp.where(j < 9, j + 1, j + 3))
+        five = jnp.where(j < 9, j + 1, j + 3)
+        six = jnp.where(j < 8, j + 1, j + 4)
+        usual = jnp.where(j < 7, j, jnp.where(low, five, six))
         return jnp.where(slow, j + SEAM_AROUND, jnp.where(last_e, j, usual))
 
     def remote(src, dst, send, recv, block):
@@ -190,7 +194,7 @@
         return remote(
             raw.at[tile_rows(p, PIECE)],
             ring.at[tile_rows(i, PIECE)],
-            near_send.at[p],
+            near_send,
             ring_sem.at[i],
             ahead,
         )
@@ -198,33 +202,33 @@
     def straight(j):
         p = direct_piece(j)
         rows = tile_rows(p, PIECE)
-        return remote(raw.at[rows], near_in.at[rows], near_send.at[p], near_sem.at[p], mate)
+        return remote(raw.at[rows], near_in.at[rows], near_send, near_sem.at[lax.div(p, UNIT // PIECE)], mate)
 
     def leg_two(i):
         rows = tile_rows(i, PIECE)
-        return remote(ring.at[rows], ring.at[rows], ring_send.at[i], ring_sem.at[i], ahead)
+        return remote(ring.at[rows], ring.at[rows], ring_send, ring_sem.at[i], ahead)
 
     def leg_three(i):
         p = around_piece(i)
         return remote(
             ring.at[tile_rows(i, PIECE)],
             near_in.at[tile_rows(p, PIECE)],
-            ring_send.at[i],
-            near_sem.at[p],
+            ring_send,
+            near_sem.at[lax.div(p, UNIT // PIECE)],
             ahead,
         )
 
     def far_copy(which, t, block):
         rows = tile_rows(t, TILE)
-        return remote(raw.at[rows], far_in.at[rows], far_send.at[which, t], far_sem.at[t], block)
+        return remote(raw.at[rows], far_in.at[rows], far_send.at[which], far_sem.at[lax.div(t, UNIT // TILE)], block)
 
     def seam_copy(t, block):
         rows = tile_rows(t, PIECE)
-        return remote(raw.at[rows], pass_on.at[rows], extra_send.at[t], pass_sem.at[t], block)
+        return remote(raw.at[rows], pass_on.at[rows], extra_send, pass_sem.at[t], block)
 
     def seam_pass(t, block):
         rows = tile_rows(t, PIECE)
-        return remote(pass_on.at[rows], extra_in.at[rows], pass_send.at[t], extra_sem.at[t], block)
+        return remote(pass_on.at[rows], extra_in.at[rows], pass_send, extra_sem.at[lax.div(t, UNIT // PIECE)], block)
 
     def each(count, body):
         def step(t, carry):
@@ -289,9 +293,9 @@
                     jnp.max(block[q * TILE : q * TILE + TILE, :], axis=0, keepdims=True) * scale
                 )
 
-    def pair_unit(keys_ref, rows_ref, u, by_row, row_base, by_key, key_base):
+    def pair_unit(keys_ref, rows_ref, u, by_row, row_base, by_key, key_base, parts=UNITS):
         left = keys_ref[tile_rows(u, UNIT), :]
-        for n in range(UNITS):
+        for n in range(parts):
             span = slice(n * UNIT, n * UNIT + UNIT)
             block = scores(left, rows_ref[span, :])
             for q in range(UNIT // TILE):
@@ -309,11 +313,9 @@
     def slot(offset):
         return pl.multiple_of((offset + 2) * TILES, TILES)
 
-    def take(landing, ref, sems, u, size):
-        for k in range(UNIT // size):
-            t = u * (UNIT // size) + k
-            rows = tile_rows(t, size)
-            pltpu.make_async_copy(raw.at[rows], landing.at[rows], sems.at[t]).wait()
+    def take(landing, ref, sems, u):
+        rows = tile_rows(u, UNIT)
+        pltpu.make_async_copy(raw.at[rows], landing.at[rows], sems.at[u]).wait()
         normalise(landing, ref, u)
 
     def message(k, block, offset):
@@ -327,13 +329,13 @@
 
     def far_unit(u):
         with jax.named_scope("farw"):
-            take(far_in, far, far_sem, u, TILE)
+            take(far_in, far, far_sem, u)
         with jax.named_scope("farc"):
             pair_unit(far, unit, u, out_ref, slot(2 * s), back, 0)
 
     def near_take(u):
         with jax.named_scope("nearw"):
-            take(near_in, near, near_sem, u, PIECE)
+            take(near_in, near, near_sem, u)
 
     def near_score(u):
         with jax.named_scope("nearc"):
@@ -349,16 +351,23 @@
 
     def extra_take(u):
         with jax.named_scope("xw"):
-            take(extra_in, extra, extra_sem, u, PIECE)
+            take(extra_in, extra, extra_sem, u)
+
+    def extra_score(u):
+        with jax.named_scope("xuc"):
+            pair_unit(extra, unit, u, out_ref, slot(1), back, 4 * TILES)
 
     def extra_unit(u):
         extra_take(u)
-        with jax.named_scope("xuc"):
-            pair_unit(extra, unit, u, out_ref, slot(1), back, 4 * TILES)
-
-    def extra_near_unit(u):
+        extra_score(u)
+
+    def extra_near_unit(u, parts=UNITS - 1):
         with jax.named_scope("xnc"):
-            pair_unit(extra, near, u, back, 5 * TILES, back, 6 * TILES)
+            pair_unit(extra, near, u, back, 5 * TILES, back, 6 * TILES, parts)
+
+    def last_near_extra(parts=UNITS):
+        with jax.named_scope("nxc"):
+            pair_unit(near, extra, UNITS - 1, back, 6 * TILES, back, 5 * TILES, parts)
 
     def seam_forward(t):
         rows = tile_rows(t, PIECE)
@@ -404,9 +413,13 @@
             with jax.named_scope("own"):
                 own_unit(i)
 
-    each(jnp.where(passes, (PIECES - LEAD) // 2, jnp.where(slow, SEAM_AROUND, AROUND)), forward)
+    each(jnp.where(slow, SEAM_AROUND, AROUND + 1), forward)
 
     plain = both(even, jnp.logical_not(cross_e))
+
+    def extra_take_near(u):
+        extra_take(u)
+        extra_near_unit(u)
 
     def arrive(k):
         @pl.when(both(even, step_in, k == 3))
@@ -417,7 +430,7 @@
         def _():
             far_unit(k)
 
-        @pl.when(both(plain, jnp.logical_or(k == 1, k == 2)))
+        @pl.when(both(plain, jnp.logical_not(slow), jnp.logical_or(k == 1, k == 2)))
         def _():
             near_unit(k - 1)
 
@@ -430,14 +443,17 @@
     @pl.when(plain)
     def _():
         def rest(k):
-            @pl.when(both(k == 2, jnp.logical_not(step_in)))
-            def _():
-                near_unit(2)
+            @pl.when(jnp.logical_or(both(k == 2, jnp.logical_not(step_in)), both(slow, k < 2)))
+            def _():
+                near_unit(k)
 
             @pl.when(both(cross_o, k == 2))
             def _():
-                extra_take(0)
-                extra_take(1)
+                each(2, extra_take_near)
+
+            @pl.when(both(cross_o, k == 3))
+            def _():
+                extra_take_near(2)
 
             @pl.when(k == 3)
             def _():
@@ -457,41 +473,38 @@
         near_score(3)
         message(1, mate, -s).start()
 
+        @pl.when(cross_o)
+        def _():
+            last_near_extra(UNITS - 1)
+            extra_take(3)
+            extra_near_unit(3, UNITS)
+            message(5, mate, -2).start()
+
     @pl.when(cross_e)
     def _():
-        def all_four(u):
+        def all_three(u):
             near_unit(u)
             near_far_unit(u)
-
-            @pl.when(u < UNITS - 1)
-            def _():
-                extra_unit(u)
-
-        each(UNITS, all_four)
+            extra_unit(u)
+
+        each(UNITS - 1, all_three)
+        each(UNITS - 1, extra_near_unit)
+        near_take(3)
+        extra_take(3)
+        extra_near_unit(3)
+        last_near_extra()
+        message(6, over, -2).start()
+        message(5, mate, 2).start()
+        extra_score(3)
+        message(4, over, -1).start()
+        near_far_unit(3)
         message(2, b + 2 * s, -s).start()
         message(3, mate, s).start()
+        near_score(3)
         message(1, mate, -s).start()
 
-    @pl.when(cross_e)
-    def _():
-        each(UNITS - 1, extra_near_unit)
-        extra_unit(UNITS - 1)
-        message(4, over, -1).start()
-        extra_near_unit(UNITS - 1)
-        message(5, mate, 2).start()
-        message(6, over, -2).start()
-
     @pl.when(cross_o)
     def _():
-        def seam_unit(u):
-            @pl.when(u >= 2)
-            def _():
-                extra_take(u)
-
-            extra_near_unit(u)
-
-        each(UNITS, seam_unit)
-        message(5, mate, -2).start()
         pl.semaphore_wait(hello, 1)
         message(6, over, 2).start()
 
@@ -518,31 +531,21 @@
             landed(2 * s)
 
     with jax.named_scope("settle"):
-        @pl.when(odd)
-        def _():
-            each(around, lambda i: leg_one(i).wait_send())
-            each(direct, lambda j: straight(j).wait_send())
-            each(around, lambda i: leg_three(i).wait_send())
-
-        @pl.when(even)
-        def _():
-            each(around, lambda i: leg_two(i).wait_send())
-
-        @pl.when(sends_far)
-        def _():
-            each(TILES, lambda t: far_copy(0, t, b - 2 * s).wait_send())
-
-        @pl.when(no_far)
-        def _():
-            each(TILES, lambda t: far_copy(1, t, b + 2 * s).wait_send())
-
-        @pl.when(cross)
-        def _():
-            each(PIECES, lambda t: seam_copy(t, seam_to).wait_send())
-
-        @pl.when(passes)
-        def _():
-            each(PIECES, lambda t: seam_pass(t, pass_to).wait_send())
+        def left(condition, sem, rows=ROWS):
+            @pl.when(condition)
+            def _():
+                part = pl.ds(0, rows)
+                pltpu.make_async_copy(raw.at[part], raw.at[part], sem).wait()
+
+        usual = jnp.logical_not(last_e)
+        left(both(usual, low), ring_send, AROUND * PIECE)
+        left(both(usual, high), ring_send, (AROUND + 1) * PIECE)
+        left(slow, ring_send, SEAM_AROUND * PIECE)
+        left(odd, near_send)
+        left(sends_far, far_send.at[0])
+        left(no_far, far_send.at[1])
+        left(cross, extra_send)
+        left(passes, pass_send)
 
         @pl.when(has_far)
         def _():
@@ -590,16 +593,16 @@
             pltpu.VMEM((SEAM_AROUND * PIECE, width), jnp.bfloat16),
             pltpu.VMEM((7 * TILES, rows), jnp.float32),
             dma,
+            dma,
+            dma((UNITS,)),
+            dma,
+            dma((SEAM_AROUND,)),
+            dma((2,)),
+            dma((UNITS,)),
+            dma,
+            dma((UNITS,)),
             dma((PIECES,)),
-            dma((PIECES,)),
-            dma((SEAM_AROUND,)),
-            dma((SEAM_AROUND,)),
-            dma((2, TILES)),
-            dma((TILES,)),
-            dma((PIECES,)),
-            dma((PIECES,)),
-            dma((PIECES,)),
-            dma((PIECES,)),
+            dma,
             dma((7,)),
             dma((5,)),
             pltpu.SemaphoreType.REGULAR,

time: 46.5 us -> 42.9 us (0.923)
  Pallas kernels: 45.7 us -> 41.8 us
    pallas_call x1, Pallas kernels: 45.7 us -> 41.8 us  [body(): pl.pallas_call(kernel, name='cycle_tile_max', out_shape=jax.ShapeDtypeStr...]
where the time goes in v5:
time: 42.9 us; the launch traced here: 42.5 us
  Pallas kernels  41.8 us (97%)
  local copies, waits for them, and re-layouts  0.67 us (2%)
    pallas_call x1, Pallas kernels, body(): pl.pallas_call(kernel, name='cycle_tile_max', out_shape=jax.ShapeDtypeStr...  41.8 us

profile of v5, /device:TPU:16, one launch (start us, length us, event | category | flops | bytes accessed | tf_op | source)
XLA Modules:
  0.0 42.5 jit_solution(9942395556292719873)
XLA Ops:
  0.0 41.8 %cycle_tile_max.1 = f32[40,1024]{1,0:T(8,128)S(1)} custom-call(bf16[1024,1024]{1,0:T(8,128)(2,1)} %x_ref.1), custom_call_target="tpu_custom_call" | custom-call | flops 8589934592 | bytes 4194304 | tf_op jit(solution)/shard_map/cycle_tile_max/pallas_call | solution.py:577
  41.9 0.7 %copy.3 = f32[1024,40]{0,1:T(8,128)} copy(f32[1024,40]{0,1:T(8,128)S(1)} %bitcast.1) | data formatting | bytes 327680

commit v6 on v5

--- a/solution.py
+++ b/solution.py
@@ -11,11 +11,12 @@
 TILES = ROWS // TILE
 UNIT = 256
 UNITS = ROWS // UNIT
-PIECE = 64
+PIECE = 32
 PIECES = ROWS // PIECE
-AROUND = 5
-SEAM_AROUND = 10
-LEAD = 4
+AROUND = 10
+SEAM_AROUND = 20
+LEAD = 8
+STEPS = (PIECES - LEAD) // 2
 GRP = 2
 BLOCKS = 256
 
@@ -168,15 +169,15 @@
         return pl.ds(pl.multiple_of(t * size, size), size)
 
     def around_piece(i):
-        five = jnp.where(i < 3, i + 9, i + 11)
-        six = jnp.where(i < 4, i + 8, i + 10)
-        usual = jnp.where(i == 0, 7, jnp.where(low, five, six))
+        fewer = jnp.where(i < 6, i + 18, i + 22)
+        more = jnp.where(i < 7, jnp.where(i < 3, 19, i + 17), i + 21)
+        usual = jnp.where(i < 2, i + 14, jnp.where(low, fewer, more))
         return jnp.where(slow, i, usual)
 
     def direct_piece(j):
-        five = jnp.where(j < 9, j + 1, j + 3)
-        six = jnp.where(j < 8, j + 1, j + 4)
-        usual = jnp.where(j < 7, j, jnp.where(low, five, six))
+        fewer = jnp.where(j < 18, j + 2, j + 6)
+        more = jnp.where(j < 17, j + 2, j + 7)
+        usual = jnp.where(j < 14, j, jnp.where(low, fewer, more))
         return jnp.where(slow, j + SEAM_AROUND, jnp.where(last_e, j, usual))
 
     def remote(src, dst, send, recv, block):
@@ -293,9 +294,9 @@
                     jnp.max(block[q * TILE : q * TILE + TILE, :], axis=0, keepdims=True) * scale
                 )
 
-    def pair_unit(keys_ref, rows_ref, u, by_row, row_base, by_key, key_base, parts=UNITS):
+    def pair_unit(keys_ref, rows_ref, u, by_row, row_base, by_key, key_base, parts=UNITS, first=0):
         left = keys_ref[tile_rows(u, UNIT), :]
-        for n in range(parts):
+        for n in range(first, parts):
             span = slice(n * UNIT, n * UNIT + UNIT)
             block = scores(left, rows_ref[span, :])
             for q in range(UNIT // TILE):
@@ -353,6 +354,10 @@
         with jax.named_scope("xw"):
             take(extra_in, extra, extra_sem, u)
 
+    def far_near_unit(u):
+        with jax.named_scope("fnc"):
+            pair_unit(far, near, u, back, 3 * TILES, back, 2 * TILES, 2)
+
     def extra_score(u):
         with jax.named_scope("xuc"):
             pair_unit(extra, unit, u, out_ref, slot(1), back, 4 * TILES)
@@ -364,6 +369,10 @@
     def extra_near_unit(u, parts=UNITS - 1):
         with jax.named_scope("xnc"):
             pair_unit(extra, near, u, back, 5 * TILES, back, 6 * TILES, parts)
+
+    def extra_near_span(u, first, parts):
+        with jax.named_scope("xns"):
+            pair_unit(extra, near, u, back, 5 * TILES, back, 6 * TILES, parts, first)
 
     def last_near_extra(parts=UNITS):
         with jax.named_scope("nxc"):
@@ -385,7 +394,7 @@
         each(LEAD, seam_forward)
 
     def forward(i):
-        @pl.when(both(passes, i < (PIECES - LEAD) // 2))
+        @pl.when(both(passes, i < STEPS))
         def _():
             seam_forward(LEAD + 2 * i)
             seam_forward(LEAD + 2 * i + 1)
@@ -404,7 +413,7 @@
             def _():
                 leg_three(i).start()
 
-        @pl.when(both(slow, odd, i == 8))
+        @pl.when(both(slow, odd, i == 16))
         def _():
             each(direct, lambda j: straight(j).start())
 
@@ -413,24 +422,35 @@
             with jax.named_scope("own"):
                 own_unit(i)
 
-    each(jnp.where(slow, SEAM_AROUND, AROUND + 1), forward)
+    each(jnp.where(slow, SEAM_AROUND, STEPS), forward)
 
     plain = both(even, jnp.logical_not(cross_e))
 
-    def extra_take_near(u):
-        extra_take(u)
-        extra_near_unit(u)
-
     def arrive(k):
+        @pl.when(both(even, step_in, k == 2))
+        def _():
+            near_unit(1)
+
         @pl.when(both(even, step_in, k == 3))
         def _():
+            each(3, far_near_unit)
             near_unit(2)
 
         @pl.when(has_far)
         def _():
             far_unit(k)
 
-        @pl.when(both(plain, jnp.logical_not(slow), jnp.logical_or(k == 1, k == 2)))
+        @pl.when(both(even, step_in, k == 3))
+        def _():
+            far_near_unit(3)
+
+        @pl.when(
+            both(
+                plain,
+                jnp.logical_not(slow),
+                jnp.logical_or(k == 1, both(k == 2, jnp.logical_not(step_in))),
+            )
+        )
         def _():
             near_unit(k - 1)
 
@@ -443,23 +463,29 @@
     @pl.when(plain)
     def _():
         def rest(k):
+            @pl.when(both(cross_o, k == 2))
+            def _():
+                each(2, extra_take)
+                each(2, lambda u: extra_near_unit(u, 2))
+
             @pl.when(jnp.logical_or(both(k == 2, jnp.logical_not(step_in)), both(slow, k < 2)))
             def _():
                 near_unit(k)
 
             @pl.when(both(cross_o, k == 2))
             def _():
-                each(2, extra_take_near)
+                each(2, lambda u: extra_near_span(u, 2, UNITS - 1))
 
             @pl.when(both(cross_o, k == 3))
             def _():
-                extra_take_near(2)
+                extra_take(2)
+                extra_near_unit(2)
 
             @pl.when(k == 3)
             def _():
                 near_take(3)
 
-            @pl.when(has_far)
+            @pl.when(both(has_far, jnp.logical_or(k >= 2, jnp.logical_not(step_in))))
             def _():
                 near_far_unit(k)
 
@@ -490,9 +516,9 @@
         each(UNITS - 1, all_three)
         each(UNITS - 1, extra_near_unit)
         near_take(3)
+        last_near_extra(UNITS - 1)
         extra_take(3)
-        extra_near_unit(3)
-        last_near_extra()
+        extra_near_unit(3, UNITS)
         message(6, over, -2).start()
         message(5, mate, 2).start()
         extra_score(3)

time: 42.9 us -> 43.2 us (level)
  Pallas kernels: 41.8 us -> 42.5 us
    pallas_call x1, Pallas kernels: 41.8 us -> 42.5 us  [body(): pl.pallas_call(kernel, name='cycle_tile_max', out_shape=jax.ShapeDtypeStr...]
where the time goes in v6:
time: 43.2 us; the launch traced here: 43.1 us
  Pallas kernels  42.5 us (98%)
  local copies, waits for them, and re-layouts  0.67 us (2%)
    pallas_call x1, Pallas kernels, body(): pl.pallas_call(kernel, name='cycle_tile_max', out_shape=jax.ShapeDtypeStr...  42.5 us

profile of v6, /device:TPU:16, one launch (start us, length us, event | category | flops | bytes accessed | tf_op | source)
XLA Modules:
  0.0 43.1 jit_solution(11710461320487045328)
XLA Ops:
  0.0 42.5 %cycle_tile_max.1 = f32[40,1024]{1,0:T(8,128)S(1)} custom-call(bf16[1024,1024]{1,0:T(8,128)(2,1)} %x_ref.1), custom_call_target="tpu_custom_call" | custom-call | flops 8589934592 | bytes 4194304 | tf_op jit(solution)/shard_map/cycle_tile_max/pallas_call | solution.py:603
  42.5 0.7 %copy.3 = f32[1024,40]{0,1:T(8,128)} copy(f32[1024,40]{0,1:T(8,128)S(1)} %bitcast.1) | data formatting | bytes 327680

commit v7 on v6

--- a/solution.py
+++ b/solution.py
@@ -413,7 +413,7 @@
             def _():
                 leg_three(i).start()
 
-        @pl.when(both(slow, odd, i == 16))
+        @pl.when(both(slow, odd, i == 18))
         def _():
             each(direct, lambda j: straight(j).start())
 

time: 43.2 us -> 42.7 us (0.988)
  Pallas kernels: 42.5 us -> 41.7 us
    pallas_call x1, Pallas kernels: 42.5 us -> 41.7 us  [body(): pl.pallas_call(kernel, name='cycle_tile_max', out_shape=jax.ShapeDtypeStr...]
where the time goes in v7:
time: 42.7 us; the launch traced here: 42.4 us
  Pallas kernels  41.7 us (98%)
  local copies, waits for them, and re-layouts  0.67 us (2%)
    pallas_call x1, Pallas kernels, body(): pl.pallas_call(kernel, name='cycle_tile_max', out_shape=jax.ShapeDtypeStr...  41.7 us

profile of v7, /device:TPU:16, one launch (start us, length us, event | category | flops | bytes accessed | tf_op | source)
XLA Modules:
  0.0 42.4 jit_solution(1029537515875051455)
XLA Ops:
  0.0 41.7 %cycle_tile_max.1 = f32[40,1024]{1,0:T(8,128)S(1)} custom-call(bf16[1024,1024]{1,0:T(8,128)(2,1)} %x_ref.1), custom_call_target="tpu_custom_call" | custom-call | flops 8589934592 | bytes 4194304 | tf_op jit(solution)/shard_map/cycle_tile_max/pallas_call | solution.py:603
  41.7 0.7 %copy.3 = f32[1024,40]{0,1:T(8,128)} copy(f32[1024,40]{0,1:T(8,128)S(1)} %bitcast.1) | data formatting | bytes 327680

commit v8 on v7

--- a/solution.py
+++ b/solution.py
@@ -413,7 +413,7 @@
             def _():
                 leg_three(i).start()
 
-        @pl.when(both(slow, odd, i == 18))
+        @pl.when(both(slow, odd, i == SEAM_AROUND - 1))
         def _():
             each(direct, lambda j: straight(j).start())
 

time: 42.7 us -> 42.7 us (level)
  no operation moved by 1% of the time
where the time goes in v8:
time: 42.7 us; the launch traced here: 42.4 us
  Pallas kernels  41.7 us (98%)
  local copies, waits for them, and re-layouts  0.67 us (2%)
    pallas_call x1, Pallas kernels, body(): pl.pallas_call(kernel, name='cycle_tile_max', out_shape=jax.ShapeDtypeStr...  41.7 us

profile of v8, /device:TPU:16, one launch (start us, length us, event | category | flops | bytes accessed | tf_op | source)
XLA Modules:
  0.0 42.4 jit_solution(366515757510104345)
XLA Ops:
  0.0 41.7 %cycle_tile_max.1 = f32[40,1024]{1,0:T(8,128)S(1)} custom-call(bf16[1024,1024]{1,0:T(8,128)(2,1)} %x_ref.1), custom_call_target="tpu_custom_call" | custom-call | flops 8589934592 | bytes 4194304 | tf_op jit(solution)/shard_map/cycle_tile_max/pallas_call | solution.py:603
  41.7 0.7 %copy.3 = f32[1024,40]{0,1:T(8,128)} copy(f32[1024,40]{0,1:T(8,128)S(1)} %bitcast.1) | data formatting | bytes 327680
